TPU v7x, 32 devices: a whole 2x2x4 slice. The times are simulated.
32 devices in a mesh: seg: 32 (over z, y, x, core).
Axes of the slice: x: 2, y: 2, z: 4, core: 2. Of those that a mesh axis runs over, the one named last changes fastest.
Arguments:
- cam_jac: bfloat16 [18, 512, 512], P(None, 'seg'), may hold values from -0.25 to 0.25
- point_jac: bfloat16 [6, 512, 512], P(None, 'seg'), may hold values from -6 to 6
- obs_point: int32 [512, 512], P('seg'), may hold values from 0 to 1791, as said below
- obs_count: int32 [512], P('seg'), may hold values from 64 to 512, as said below
- back_list: int32 [32, 384], P('seg'), may hold values from 0 to 1023, as said below
- front_list: int32 [32, 384], P('seg'), may hold values from 0 to 1023, as said below
- point_damp: float32 [32768], P('seg'), may hold values from 0.5 to 4
- cam_damp: float32 [512], P('seg'), may hold values from 0.1 to 1
- right_side: float32 [9, 512], P(None, 'seg'), may hold values from -25 to 25
- start_guess: float32 [9, 512], P(None, 'seg'), may hold values from -3 to 3
Outputs:
- camera_step: float32 [9, 512], P(None, 'seg')
- residual: float32 [9, 512], P(None, 'seg')
Inputs may be any that keep to these rules, and one draw needn't show every extreme that they name: `obs_point`: entries below 1024 name the segment's own points; an entry e from 1024 to 1407 names entry e - 1024 of the previous segment's back_list, and a larger one entry e - 1408 of the next segment's front_list. Keyframes of the first segment name no back slot, those of the last segment no front slot. `obs_count`: slots at or past a keyframe's count are padding. Every segment has a keyframe whose slots are all used. `back_list`: each row holds 384 distinct own points of the segment; no point stands on both lists of its segment. `front_list`: each row holds 384 distinct own points of the segment; no point stands on both lists of its segment.
All inputs are finite; a program needn't handle non-finite values.
Results may differ from a plain program's by a relative error of at most 0.0005.
Values sent between devices are 32-bit elements; how exact they have to be, the bound alone decides.
A program may use at most 64 MiB of HBM per device.

v0:
```python
import jax
import jax.numpy as jnp
from jax import lax
from jax.sharding import PartitionSpec as P

ITERS = 2


ENTRY_PAIRS = ((0, 0), (0, 1), (0, 2), (1, 1), (1, 2), (2, 2))


def padded(block, sides, width):
    for axis, dim in sides:
        count = lax.axis_size(axis)
        forward = [(i, i + 1) for i in range(count - 1)]
        backward = [(target, source) for source, target in forward]
        low = lax.ppermute(
            lax.slice_in_dim(block, block.shape[dim] - width, None, axis=dim), axis, forward
        )
        high = lax.ppermute(lax.slice_in_dim(block, 0, width, axis=dim), axis, backward)
        block = jnp.concatenate([low, block, high], axis=dim)
    return block


def slot_weights(obs_count, slot_total):
    positions = lax.broadcasted_iota(jnp.int32, (obs_count.shape[0], slot_total), 1)
    return (positions < obs_count[:, None]).astype(jnp.float32)


def symmetric_inverse(entries):
    cofactors = [
        entries[3] * entries[5] - entries[4] * entries[4],
        entries[2] * entries[4] - entries[1] * entries[5],
        entries[1] * entries[4] - entries[2] * entries[3],
        entries[0] * entries[5] - entries[2] * entries[2],
        entries[1] * entries[2] - entries[0] * entries[4],
        entries[0] * entries[3] - entries[1] * entries[1],
    ]
    determinant = entries[0] * cofactors[0] + entries[1] * cofactors[1] + entries[2] * cofactors[2]
    determinant = jnp.where(determinant > 0.0, determinant, 1.0)
    return jnp.stack([member / determinant for member in cofactors])


def apply_inverse(inverse, point_sums):
    return jnp.stack(
        [
            inverse[0] * point_sums[0] + inverse[1] * point_sums[1] + inverse[2] * point_sums[2],
            inverse[1] * point_sums[0] + inverse[3] * point_sums[1] + inverse[4] * point_sums[2],
            inverse[2] * point_sums[0] + inverse[4] * point_sums[1] + inverse[5] * point_sums[2],
        ]
    )


def camera_rows(cam_jac, vector, weights):
    error_rows = []
    for row_index in range(2):
        running = cam_jac[9 * row_index].astype(jnp.float32) * vector[0][:, None]
        for column in range(1, 9):
            running = (
                running
                + cam_jac[9 * row_index + column].astype(jnp.float32) * vector[column][:, None]
            )
        error_rows.append(running * weights)
    return error_rows


def both_outgoing(own_sums, slot_sums, back_ids, front_ids, border):
    return jnp.concatenate(
        [
            slot_sums[:, :border],
            own_sums[:, front_ids],
            own_sums[:, back_ids],
            slot_sums[:, border:],
        ],
        axis=1,
    )


def fold_both(own_sums, slot_sums, received, back_ids, front_ids, border):
    from_before = received[:, : 2 * border]
    from_after = received[:, 6 * border :]
    own_complete = (
        own_sums.at[:, front_ids]
        .add(from_before[:, border:])
        .at[:, back_ids]
        .add(from_after[:, :border])
    )
    back_complete = slot_sums[:, :border] + from_before[:, :border]
    front_complete = slot_sums[:, border:] + from_after[:, border:]
    return jnp.concatenate([own_complete, back_complete, front_complete], axis=1)


def shards(
    cam_jac,
    point_jac,
    obs_point,
    obs_count,
    back_list,
    front_list,
    point_damp,
    cam_damp,
    right_side,
    start_guess,
):
    cameras, slot_total = obs_point.shape
    points = point_damp.shape[0]
    border = back_list.shape[1]
    extended = points + 2 * border
    weights = slot_weights(obs_count, slot_total)
    owners = obs_point.reshape(-1)
    back_ids = back_list[0]
    front_ids = front_list[0]
    partial_value = []
    damping = []
    for lead_index, tail_index in ENTRY_PAIRS:
        product = point_jac[lead_index].astype(jnp.float32) * point_jac[tail_index].astype(
            jnp.float32
        )
        product = product + point_jac[3 + lead_index].astype(jnp.float32) * point_jac[
            3 + tail_index
        ].astype(jnp.float32)
        partial_value.append(
            jax.ops.segment_sum((product * weights).reshape(-1), owners, num_segments=extended)
        )
        damping.append(point_damp if lead_index == tail_index else jnp.zeros_like(point_damp))
    partial_value = jnp.stack(partial_value)
    own_part = partial_value[:, :points] + jnp.stack(damping)
    outgoing = both_outgoing(own_part, partial_value[:, points:], back_ids, front_ids, border)
    received = padded(outgoing, (("seg", 1),), 2 * border)
    inverse = symmetric_inverse(
        fold_both(own_part, partial_value[:, points:], received, back_ids, front_ids, border)
    )
    diagonal = []
    for column in range(9):
        squared = (
            cam_jac[column].astype(jnp.float32) ** 2 + cam_jac[9 + column].astype(jnp.float32) ** 2
        )
        diagonal.append(jnp.sum(squared * weights, axis=1) + cam_damp)
    precond = 1.0 / jnp.stack(diagonal)

    def operator(vector):
        errors = camera_rows(cam_jac, vector, weights)
        point_sums = []
        for column in range(3):
            product = errors[0] * point_jac[column].astype(jnp.float32) + errors[1] * point_jac[
                3 + column
            ].astype(jnp.float32)
            point_sums.append(
                jax.ops.segment_sum(product.reshape(-1), owners, num_segments=extended)
            )
        point_sums = jnp.stack(point_sums)
        outgoing = both_outgoing(
            point_sums[:, :points], point_sums[:, points:], back_ids, front_ids, border
        )
        received = padded(outgoing, (("seg", 1),), 2 * border)
        values = apply_inverse(
            inverse,
            fold_both(
                point_sums[:, :points],
                point_sums[:, points:],
                received,
                back_ids,
                front_ids,
                border,
            ),
        )
        picked = values[:, owners].reshape(3, cameras, slot_total)
        adjusted = []
        for row_index in range(2):
            back_term = picked[0] * point_jac[3 * row_index].astype(jnp.float32)
            back_term = back_term + picked[1] * point_jac[3 * row_index + 1].astype(jnp.float32)
            back_term = back_term + picked[2] * point_jac[3 * row_index + 2].astype(jnp.float32)
            adjusted.append(errors[row_index] - weights * back_term)
        result = []
        for column in range(9):
            running = jnp.sum(
                cam_jac[column].astype(jnp.float32) * adjusted[0]
                + cam_jac[9 + column].astype(jnp.float32) * adjusted[1],
                axis=1,
            )
            result.append(cam_damp * vector[column] + running)
        return jnp.stack(result)

    def squares(residual, scaled):
        return lax.psum(jnp.sum(residual * scaled), "seg")

    solution = start_guess
    residual = right_side - operator(solution)
    scaled = precond * residual
    direction = scaled
    inner_now = squares(residual, scaled)
    for iteration in range(ITERS):
        image = operator(direction)
        step_size = inner_now / lax.psum(jnp.sum(direction * image), "seg")
        solution = solution + step_size * direction
        residual = residual - step_size * image
        if iteration + 1 < ITERS:
            scaled = precond * residual
            inner_next = squares(residual, scaled)
            direction = scaled + inner_next / inner_now * direction
            inner_now = inner_next
    return (solution, residual)


def solution(mesh):
    return jax.shard_map(
        shards,
        mesh=mesh,
        in_specs=(
            P(None, "seg", None),
            P(None, "seg", None),
            P("seg", None),
            P("seg"),
            P("seg", None),
            P("seg", None),
            P("seg"),
            P("seg"),
            P(None, "seg"),
            P(None, "seg"),
        ),
        out_specs=(P(None, "seg"), P(None, "seg")),
        check_vma=False,
    )
```

profile of v0, /device:TPU:0, one launch (start us, length us, event | category | flops | bytes accessed | tf_op | source)
XLA Modules:
  0.0 997.7 jit_solution(2922983266211427238)
XLA Ops:
  0.6 1.0 slice_bitcast_fusion.34
  1.6 0.7 fusion.303
  2.5 0.8 copy.61
  3.7 0.8 convert_bitcast_fusion.25
  4.6 1.0 convert_bitcast_fusion.17
  6.1 46.4 %scatter_custom_fusion.5 = f32[1792]{0:T(1024)S(1)} fusion(s32[8192]{0:T(1024)S(1)} %bitcast.1428, f32[8192]{0:T(1024)S(1)} %get-tuple-element.124, f32[]{:T(128)} %constant.37.clone.1), kind=kCustom, calls=%fused_computation.548 | custom fusion | flops 8192 | bytes 7172 | tf_op jit(solution)/shard_map/scatter-add | solution.py:123
  52.5 46.4 %scatter_custom_fusion.4 = f32[1792]{0:T(1024)S(1)} fusion(s32[8192]{0:T(1024)S(1)} %bitcast.1429, f32[8192]{0:T(1024)S(1)} %get-tuple-element.125, f32[]{:T(128)} %constant.37.clone.1), kind=kCustom, calls=%fused_computation.550 | custom fusion | flops 8192 | bytes 7172 | tf_op jit(solution)/shard_map/scatter-add | solution.py:123
  98.9 46.4 %scatter_custom_fusion.3 = f32[1792]{0:T(1024)S(1)} fusion(s32[8192]{0:T(1024)S(1)} %bitcast.1430, f32[8192]{0:T(1024)S(1)} %get-tuple-element.126, f32[]{:T(128)} %constant.37.clone.1), kind=kCustom, calls=%fused_computation.552 | custom fusion | flops 8192 | bytes 7172 | tf_op jit(solution)/shard_map/scatter-add | solution.py:123
  145.3 46.4 %scatter_custom_fusion.1 = f32[1792]{0:T(1024)S(1)} fusion(s32[8192]{0:T(1024)S(1)} %bitcast.1431, f32[8192]{0:T(1024)S(1)} %get-tuple-element.127, f32[]{:T(128)} %constant.37.clone.1), kind=kCustom, calls=%fused_computation.556 | custom fusion | flops 8192 | bytes 7172 | tf_op jit(solution)/shard_map/scatter-add | solution.py:123
  191.6 46.4 %scatter_custom_fusion.2 = f32[1792]{0:T(1024)S(1)} fusion(s32[8192]{0:T(1024)S(1)} %bitcast.1432, f32[8192]{0:T(1024)S(1)} %get-tuple-element.128, f32[]{:T(128)} %constant.37.clone.1), kind=kCustom, calls=%fused_computation.554 | custom fusion | flops 8192 | bytes 7172 | tf_op jit(solution)/shard_map/scatter-add | solution.py:123
  238.0 46.4 %scatter_custom_fusion = f32[1792]{0:T(1024)S(1)} fusion(s32[8192]{0:T(1024)S(1)} %bitcast.1433, f32[8192]{0:T(1024)S(1)} %get-tuple-element.129, f32[]{:T(128)} %constant.37.clone.1), kind=kCustom, calls=%fused_computation.558 | custom fusion | flops 8192 | bytes 7172 | tf_op jit(solution)/shard_map/scatter-add | solution.py:123
  285.2 1.1 gather_fusion.1
  286.4 1.3 collective-permute-start.1
  287.7 1.1 gather_fusion
  289.0 3.0 collective-permute-start
  292.0 46.4 %scatter_custom_fusion.8 = f32[1792]{0:T(1024)S(1)} fusion(s32[8192]{0:T(1024)S(1)} %bitcast.1434, f32[8192]{0:T(1024)S(1)} %get-tuple-element.97, f32[]{:T(128)} %constant.37.clone.1), kind=kCustom, calls=%fused_computation.546 | custom fusion | flops 8192 | bytes 7172 | tf_op jit(solution)/shard_map/scatter-add | solution.py:149
  338.4 46.6 %scatter_custom_fusion.9 = f32[1792]{0:T(1024)S(1)} fusion(s32[8192]{0:T(1024)S(1)} %bitcast.1435, f32[8192]{0:T(1024)S(1)} %get-tuple-element.130, f32[]{:T(128)} %constant.37.clone.1), kind=kCustom, calls=%fused_computation.544 | custom fusion | flops 8192 | bytes 7172 | tf_op jit(solution)/shard_map/scatter-add | solution.py:149
  385.0 46.4 %scatter_custom_fusion.10 = f32[1792]{0:T(1024)S(1)} fusion(s32[8192]{0:T(1024)S(1)} %bitcast.1436, f32[8192]{0:T(1024)S(1)} %get-tuple-element.131, f32[]{:T(128)} %constant.37.clone.1), kind=kCustom, calls=%fused_computation.542 | custom fusion | flops 8192 | bytes 7172 | tf_op jit(solution)/shard_map/scatter-add | solution.py:149
  431.7 1.1 gather_fusion.2
  432.9 1.3 collective-permute-start.2
  434.2 0.3 fusion.250
  434.7 1.1 gather_fusion.3
  436.0 1.3 collective-permute-start.3
  437.5 2.8 scatter_fusion.2
  440.6 2.8 scatter_fusion
  443.5 2.8 scatter_fusion.1
  446.6 3.2 scatter_fusion.3
  450.3 0.3 copy.43
  450.6 27.7 %gather_fusion.4 = f32[8192,3]{1,0:T(8,128)} fusion(f32[3,1792]{0,1:T(8,128)S(1)} %copy.43, s32[8192]{0:T(1024)S(1)} %broadcast_clamp_fusion), kind=kCustom, calls=%fused_computation.4 | custom fusion | bytes 229376 | tf_op jit(solution)/shard_map/gather | solution.py:167
  478.3 10.2 %slice_reduce_fusion.6 = (f32[8192]{0:T(1024)S(1)}, f32[8192]{0:T(1024)S(1)}, f32[8192]{0:T(1024)S(1)}) fusion(f32[3,8192]{0,1:T(8,128)} %bitcast.1306), kind=kLoop, calls=%fused_computation.40 | loop fusion | bytes 196608 | tf_op jit(solution)/shard_map/slice | solution.py:172
  488.6 0.4 fusion.247
  490.0 46.4 %scatter_custom_fusion.13 = f32[1792]{0:T(1024)S(1)} fusion(s32[8192]{0:T(1024)S(1)} %bitcast.1437, f32[8192]{0:T(1024)S(1)} %get-tuple-element.69, f32[]{:T(128)} %constant.37.clone.1), kind=kCustom, calls=%fused_computation.540 | custom fusion | flops 8192 | bytes 7172 | tf_op jit(solution)/shard_map/scatter-add | solution.py:149
  536.4 46.4 %scatter_custom_fusion.14 = f32[1792]{0:T(1024)S(1)} fusion(s32[8192]{0:T(1024)S(1)} %bitcast.1438, f32[8192]{0:T(1024)S(1)} %get-tuple-element.134, f32[]{:T(128)} %constant.37.clone.1), kind=kCustom, calls=%fused_computation.538 | custom fusion | flops 8192 | bytes 7172 | tf_op jit(solution)/shard_map/scatter-add | solution.py:149
  582.8 46.4 %scatter_custom_fusion.15 = f32[1792]{0:T(1024)S(1)} fusion(s32[8192]{0:T(1024)S(1)} %bitcast.1439, f32[8192]{0:T(1024)S(1)} %get-tuple-element.135, f32[]{:T(128)} %constant.37.clone.1), kind=kCustom, calls=%fused_computation.536 | custom fusion | flops 8192 | bytes 7172 | tf_op jit(solution)/shard_map/scatter-add | solution.py:149
  629.5 1.1 gather_fusion.5
  630.7 1.3 collective-permute-start.4
  632.0 1.1 gather_fusion.6
  633.3 1.3 collective-permute-start.5
  634.7 3.0 scatter_fusion.4
  637.9 2.8 scatter_fusion.5
  641.1 0.3 copy.50
  641.4 27.7 %gather_fusion.7 = f32[8192,3]{1,0:T(8,128)} fusion(f32[3,1792]{0,1:T(8,128)S(1)} %copy.50, s32[8192]{0:T(1024)S(1)} %broadcast_clamp_fusion), kind=kCustom, calls=%fused_computation.7 | custom fusion | bytes 229376 | tf_op jit(solution)/shard_map/gather | solution.py:167
  669.1 10.1 %slice_reduce_fusion.3 = (f32[8192]{0:T(1024)S(1)}, f32[8192]{0:T(1024)S(1)}, f32[8192]{0:T(1024)S(1)}) fusion(f32[3,8192]{0,1:T(8,128)} %bitcast.1307), kind=kLoop, calls=%fused_computation.37 | loop fusion | bytes 196608 | tf_op jit(solution)/shard_map/slice | solution.py:172
  679.3 0.4 fusion.252
  679.8 0.6 multiply_reduce_fusion.2
  680.5 40.1 %all-reduce = (f32[]{:T(128)}, f32[]{:T(128)}) all-reduce(f32[]{:T(128)} %get-tuple-element.45, f32[]{:T(128)} %get-tuple-element.44), channel_id=1, replica_groups=mesh['seg'=32] {'seg'}, use_global_device_ids=true, to_apply=%region_32.33 | all-reduce | flops 2 | bytes 16 | tf_op jit(solution)/shard_map/psum | solution.py:185
  721.9 0.6 multiply_reduce_fusion.1
  722.5 41.2 %psum.30 = f32[]{:T(128)} all-reduce(f32[]{:T(128)} %get-tuple-element.59), channel_id=1, replica_groups=mesh['seg'=32] {'seg'}, use_global_device_ids=true, to_apply=%region_50.51 | all-reduce | flops 1 | bytes 8 | tf_op jit(solution)/shard_map/psum | solution.py:185
  765.9 46.4 %scatter_custom_fusion.18 = f32[1792]{0:T(1024)S(1)} fusion(s32[8192]{0:T(1024)S(1)} %bitcast.1440, f32[8192]{0:T(1024)S(1)} %get-tuple-element.56, f32[]{:T(128)} %constant.37.clone.1), kind=kCustom, calls=%fused_computation.534 | custom fusion | flops 8192 | bytes 7172 | tf_op jit(solution)/shard_map/scatter-add | solution.py:149
  812.3 46.4 %scatter_custom_fusion.19 = f32[1792]{0:T(1024)S(1)} fusion(s32[8192]{0:T(1024)S(1)} %bitcast.1441, f32[8192]{0:T(1024)S(1)} %get-tuple-element.132, f32[]{:T(128)} %constant.37.clone.1), kind=kCustom, calls=%fused_computation.532 | custom fusion | flops 8192 | bytes 7172 | tf_op jit(solution)/shard_map/scatter-add | solution.py:149
  858.7 46.4 %scatter_custom_fusion.20 = f32[1792]{0:T(1024)S(1)} fusion(s32[8192]{0:T(1024)S(1)} %bitcast.1442, f32[8192]{0:T(1024)S(1)} %get-tuple-element.133, f32[]{:T(128)} %constant.37.clone.1), kind=kCustom, calls=%fused_computation.530 | custom fusion | flops 8192 | bytes 7172 | tf_op jit(solution)/shard_map/scatter-add | solution.py:149
  905.4 1.1 gather_fusion.8
  906.6 1.3 collective-permute-start.6
  907.9 1.1 gather_fusion.9
  909.2 1.3 collective-permute-start.7
  910.6 2.8 scatter_fusion.6
  913.7 3.1 scatter_fusion.7
  917.4 27.7 %gather_fusion.10 = f32[8192,3]{1,0:T(8,128)} fusion(f32[3,1792]{0,1:T(8,128)S(1)} %copy.57, s32[8192]{0:T(1024)S(1)} %broadcast_clamp_fusion), kind=kCustom, calls=%fused_computation.10 | custom fusion | bytes 229376 | tf_op jit(solution)/shard_map/gather | solution.py:167
  945.1 10.1 %slice_reduce_fusion = (f32[8192]{0:T(1024)S(1)}, f32[8192]{0:T(1024)S(1)}, f32[8192]{0:T(1024)S(1)}) fusion(f32[3,8192]{0,1:T(8,128)} %bitcast.1305), kind=kLoop, calls=%fused_computation.34 | loop fusion | bytes 196608 | tf_op jit(solution)/shard_map/slice | solution.py:172
  955.3 0.4 fusion.254
  955.8 0.6 multiply_reduce_fusion
  956.4 38.3 %psum.31 = f32[]{:T(128)} all-reduce(f32[]{:T(128)} %multiply_reduce_fusion), channel_id=1, replica_groups=mesh['seg'=32] {'seg'}, use_global_device_ids=true, to_apply=%region_66.67 | all-reduce | flops 1 | bytes 8 | tf_op jit(solution)/shard_map/psum | solution.py:194
  996.1 0.6 multiply_add_fusion.9
  996.7 0.6 multiply_subtract_fusion
  (222 shorter events, 8.4 us)
Async XLA Ops:
  0.6 283.9 %copy-start.8 = (s32[1,384]{1,0:T(1,128)S(1)}, s32[1,384]{1,0:T(1,128)}, u32[]{:S(2)}) copy-start(s32[1,384]{1,0:T(1,128)} %param.15) | copy-start | bytes 4612
  0.6 283.9 %copy-start.4 = (f32[1024]{0:T(1024)S(1)}, f32[1024]{0:T(1024)}, u32[]{:S(2)}) copy-start(f32[1024]{0:T(1024)} %param.16) | copy-start | bytes 12292
  3.5 284.2 %copy-start.9 = (s32[1,384]{1,0:T(1,128)S(1)}, s32[1,384]{1,0:T(1,128)}, u32[]{:S(2)}) copy-start(s32[1,384]{1,0:T(1,128)} %param.14) | copy-start | bytes 4612
  4.6 429.6 %copy-start = (bf16[18,16,512]{2,1,0:T(8,128)(2,1)S(1)}, bf16[18,16,512]{2,1,0:T(8,128)(2,1)}, u32[]{:S(2)}) copy-start(bf16[18,16,512]{2,1,0:T(8,128)(2,1)} %param.10) | copy-start | bytes 884740
  4.6 429.6 %copy-start.5 = (s32[16]{0:T(128)S(1)}, s32[16]{0:T(128)}, u32[]{:S(2)}) copy-start(s32[16]{0:T(128)} %param.13) | copy-start | bytes 196
  5.6 428.9 %copy-start.2 = (s32[16,512]{1,0:T(8,128)S(1)}, s32[16,512]{1,0:T(8,128)}, u32[]{:S(2)}) copy-start(s32[16,512]{1,0:T(8,128)} %param.12) | copy-start | bytes 98308
  5.6 429.0 %copy-start.7 = (f32[16]{0:T(128)S(1)}, f32[16]{0:T(128)}, u32[]{:S(2)}) copy-start(f32[16]{0:T(128)} %param.17) | copy-start | bytes 196
  286.4 153.9 %collective-permute-start.1 = (f32[6,768]{1,0:T(8,128)S(1)}, f32[6,768]{1,0:T(8,128)S(1)}, u32[]{:S(2)}, u32[]{:S(2)}) collective-permute-start(f32[6,768]{1,0:T(8,128)S(1)} %pad_maximum_fusion.7), channel_id=1, source_target_pairs={{1,0},{2,1},{3,2},{4,3},{5,4},{6,5},{7,6},{8,7},{9,8},{10,9},{11,1... | collective-permute-start | bytes 55304 | tf_op jit(solution)/shard_map/ppermute | solution.py:20
  289.0 151.3 %collective-permute-start = (f32[6,768]{1,0:T(8,128)S(1)}, f32[6,768]{1,0:T(8,128)S(1)}, u32[]{:S(2)}, u32[]{:S(2)}) collective-permute-start(f32[6,768]{1,0:T(8,128)S(1)} %pad_maximum_fusion.6), channel_id=1, source_target_pairs={{0,1},{1,2},{2,3},{3,4},{4,5},{5,6},{6,7},{7,8},{8,9},{9,10},{10,1... | collective-permute-start | bytes 55304 | tf_op jit(solution)/shard_map/ppermute | solution.py:17
  432.9 3.1 collective-permute-start.2
  436.0 10.5 %collective-permute-start.3 = (f32[3,768]{1,0:T(4,128)S(1)}, f32[3,768]{1,0:T(4,128)S(1)}, u32[]{:S(2)}, u32[]{:S(2)}) collective-permute-start(f32[3,768]{1,0:T(4,128)S(1)} %pad_maximum_fusion.9), channel_id=1, source_target_pairs={{1,0},{2,1},{3,2},{4,3},{5,4},{6,5},{7,6},{8,7},{9,8},{10,9},{11,1... | collective-permute-start | bytes 27656 | tf_op jit(solution)/shard_map/ppermute | solution.py:20
  478.3 10.2 %copy-start.1 = (bf16[6,16,512]{2,1,0:T(8,128)(2,1)S(1)}, bf16[6,16,512]{2,1,0:T(8,128)(2,1)}, u32[]{:S(2)}) copy-start(bf16[6,16,512]{2,1,0:T(8,128)(2,1)} %param.11) | copy-start | bytes 294916
  478.3 10.7 %copy-start.3 = (f32[9,16]{1,0:T(8,128)S(1)}, f32[9,16]{1,0:T(8,128)}, u32[]{:S(2)}) copy-start(f32[9,16]{1,0:T(8,128)} %param.19) | copy-start | bytes 1732
  478.3 10.8 %copy-start.6 = (f32[9,16]{1,0:T(8,128)S(1)}, f32[9,16]{1,0:T(8,128)}, u32[]{:S(2)}) copy-start(f32[9,16]{1,0:T(8,128)} %param.18) | copy-start | bytes 1732
  630.7 2.5 collective-permute-start.4
  633.3 4.5 collective-permute-start.5
  906.6 2.5 collective-permute-start.6
  909.2 4.3 collective-permute-start.7
where the time goes:
time: 1010 us; the launch traced here: 998 us
  other arithmetic  728 us (72%)
  local copies, waits for them, and re-layouts  132 us (13%)
  blocking collectives  120 us (12%)
  starting transfers between devices  12.1 us (1%)
    scatter-add x9, other arithmetic, operator(): jax.ops.segment_sum(product.reshape(-1), owners, num_segments=extended)  417 us
    scatter-add x6, other arithmetic, shards(): jax.ops.segment_sum((product * weights).reshape(-1), owners, num_segments...  278 us
    gather x3, local copies, waits for them, and re-layouts, operator(): picked = values[:, owners].reshape(3, cameras, slot_total)  83.1 us
    psum x2, blocking collectives, squares(): return lax.psum(jnp.sum(residual * scaled), 'seg')  81.3 us
    psum x1, blocking collectives, shards(): step_size = inner_now / lax.psum(jnp.sum(direction * image), 'seg')  38.3 us
    slice x3, local copies, waits for them, and re-layouts, operator(): picked[2] * point_jac[3 * row_index + 2].astype(jnp.float32)  30.5 us
    scatter-add x8, other arithmetic, fold_both(): own_complete = own_sums.at[:, front_ids].add(from_before[:, border:]).at[...  23.4 us
  transfers between devices with their start and end apart: 8, of which 0 were waited for; matrix products, arithmetic and copies ran while one was open for 16% of the time, Pallas kernels for 0%

commit v1 on v0

v1 whole, which is shorter than its diff:
```python
import functools

import jax
import jax.numpy as jnp
from jax import lax
from jax.experimental import pallas as pl
from jax.experimental.pallas import tpu as pltpu
from jax.sharding import PartitionSpec as P

ENTRY_PAIRS = ((0, 0), (0, 1), (0, 2), (1, 1), (1, 2), (2, 2))
F32, BF16, I32 = jnp.float32, jnp.bfloat16, jnp.int32
MESH = pl.DeviceIdType.MESH
LANES = 128
WIDE = 256
GROUP = 8
SPLITS = 3
FIRST_ROWS = (0, 9, 12)


def splits_of(value):
    terms = []
    for step in range(SPLITS):
        term = value.astype(BF16).astype(F32)
        terms.append(term)
        value = value - term
    return terms


def iota(shape, dim):
    return lax.broadcasted_iota(I32, shape, dim)


def dot_nt(left, right):
    return lax.dot_general(left, right, (((1,), (1,)), ((), ())), preferred_element_type=F32)


def symmetric_inverse(entries):
    cofactors = [
        entries[3] * entries[5] - entries[4] * entries[4],
        entries[2] * entries[4] - entries[1] * entries[5],
        entries[1] * entries[4] - entries[2] * entries[3],
        entries[0] * entries[5] - entries[2] * entries[2],
        entries[1] * entries[2] - entries[0] * entries[4],
        entries[0] * entries[3] - entries[1] * entries[1],
    ]
    determinant = entries[0] * cofactors[0] + entries[1] * cofactors[1] + entries[2] * cofactors[2]
    determinant = jnp.where(determinant > 0.0, determinant, 1.0)
    return [member / determinant for member in cofactors]


def apply_inverse(inverse, sums):
    return [
        inverse[0] * sums[0] + inverse[1] * sums[1] + inverse[2] * sums[2],
        inverse[1] * sums[0] + inverse[3] * sums[1] + inverse[4] * sums[2],
        inverse[2] * sums[0] + inverse[4] * sums[1] + inverse[5] * sums[2],
    ]


def kernel(
    n,
    cam_jac,
    point_jac,
    obs_point,
    obs_count,
    back_list,
    front_list,
    point_damp,
    cam_damp,
    right_side,
    start_guess,
    step_out,
    residual_out,
    lane_hot,
    spread,
    group_of,
    picked,
    to_next,
    to_prev,
    from_prev,
    from_next,
    dots_out,
    dots_in,
    next_send,
    next_recv,
    prev_send,
    prev_recv,
    dots_send,
    dots_recv,
):
    cams, slots = obs_point.shape
    points = point_damp.shape[1]
    border = back_list.shape[1]
    edge = border // LANES
    own_groups = points // WIDE
    me = lax.axis_index("seg")

    barrier = pltpu.get_barrier_semaphore()

    def greet(offset, carry):
        pl.semaphore_signal(
            barrier, inc=1, device_id=(lax.rem(me + offset, n),), device_id_type=MESH
        )
        return carry

    from_prev[...] = jnp.zeros_like(from_prev)
    from_next[...] = jnp.zeros_like(from_next)
    lax.fori_loop(1, n, greet, 0)

    listed = jnp.concatenate([back_list[...], front_list[...]], axis=1)
    total = 2 * border
    place = iota((1, total), 1)
    in_front = place >= border
    place = jnp.where(in_front, place - border, place)
    list_group = jnp.where(in_front, edge, 0) + lax.shift_right_logical(place, 7)
    list_lane = jnp.where(in_front, LANES, 0) + (place & (LANES - 1))
    row = iota((2 * own_groups, total), 0)
    code = jnp.where(row < own_groups, list_group + 1, list_lane)
    wanted = jnp.where(row < own_groups, row, row - own_groups)
    code = jnp.where(lax.shift_right_logical(listed, 8) == wanted, code, 0)
    hot = jnp.where(iota((WIDE, total), 0) == (listed & (WIDE - 1)), 1.0, 0.0).astype(BF16)
    table = dot_nt(code.astype(F32).astype(BF16), hot)
    table_group = table[:own_groups]
    table_lane = table[own_groups:]
    other = jnp.where(table_group == 0.0, 1.0, 0.0)
    before = jnp.where(iota((WIDE, WIDE), 0) < iota((WIDE, WIDE), 1), 1.0, 0.0).astype(BF16)
    rank = jnp.dot(other.astype(BF16), before, preferred_element_type=F32)
    counts = jnp.sum(other, axis=1, keepdims=True)
    table_row = iota((own_groups, WIDE), 0)
    for index in range(own_groups - 1):
        rank = rank + jnp.where(table_row > index, counts[index : index + 1], 0.0)
    rank = rank.astype(I32)
    is_other = other > 0.0
    table_group = jnp.where(
        is_other, (2 * edge + lax.shift_right_logical(rank, 8)).astype(F32), table_group - 1.0
    )
    table_lane = jnp.where(is_other, (rank & (WIDE - 1)).astype(F32), table_lane)
    table = jnp.concatenate([table_group, table_lane], axis=0).astype(BF16)

    eye = iota((cams, cams), 0) == iota((cams, cams), 1)

    def column(line):
        wide = jnp.broadcast_to(line, (cams, cams))
        return jnp.sum(jnp.where(eye, wide, jnp.zeros_like(wide)), axis=1, keepdims=True)

    def line(col):
        wide = jnp.broadcast_to(col, (cams, cams))
        return jnp.sum(jnp.where(eye, wide, 0.0), axis=0, keepdims=True)

    used_count = column(obs_count[...].astype(F32)).astype(I32)
    used = iota((cams, slots), 1) < used_count

    ids = obs_point[...]
    back_slot = ids - points
    front_slot = back_slot - border
    own = ids < points
    in_back = ids < points + border
    side_group = jnp.where(
        in_back, lax.shift_right_logical(back_slot, 7), edge + lax.shift_right_logical(front_slot, 7)
    )
    side_lane = jnp.where(
        in_back, LANES + (back_slot & (LANES - 1)), front_slot & (LANES - 1)
    )
    old_group = lax.shift_right_logical(ids, 8)
    old_lane = ids & (WIDE - 1)
    wide_row = iota((WIDE, slots), 0)
    look_row = iota((2 * own_groups, slots), 0)
    look_row = jnp.where(look_row < own_groups, look_row, look_row - own_groups)
    for cam in range(cams):
        pick = slice(cam, cam + 1)
        hot = jnp.where(wide_row == old_lane[pick], 1.0, 0.0).astype(BF16)
        found = jnp.dot(table, hot, preferred_element_type=F32)
        found = jnp.where(look_row == old_group[pick], found, 0.0)
        new_group = jnp.sum(found[:own_groups], axis=0, keepdims=True).astype(I32)
        new_lane = jnp.sum(found[own_groups:], axis=0, keepdims=True).astype(I32)
        new_group = jnp.where(own[pick], new_group, side_group[pick])
        new_lane = jnp.where(own[pick], new_lane, side_lane[pick])
        group_of[pick] = jnp.where(used[pick], new_group, -1)
        lane_hot[:, cam * slots : (cam + 1) * slots] = jnp.where(
            wide_row == new_lane, 1.0, 0.0
        ).astype(BF16)

    group_row = iota((GROUP, slots), 0)

    def point_sums(values):
        rows = len(values) * GROUP
        terms = [splits_of(value) for value in values]
        for cam in range(cams):
            mask = group_row == group_of[cam : cam + 1]
            blocks = [
                jnp.where(mask, terms[index][step][cam : cam + 1], 0.0)
                for step in range(SPLITS)
                for index in range(len(values))
            ]
            spread[: SPLITS * rows, cam * slots : (cam + 1) * slots] = jnp.concatenate(
                blocks, axis=0
            ).astype(BF16)
        sums = dot_nt(spread[: SPLITS * rows], lane_hot[...])
        whole = sums[(SPLITS - 1) * rows :]
        for step in reversed(range(SPLITS - 1)):
            whole = whole + sums[step * rows : (step + 1) * rows]
        return [whole[index * GROUP : (index + 1) * GROUP] for index in range(len(values))]

    def neighbour(where, turn, size):
        spot = FIRST_ROWS[turn]
        if where == "next":
            return pltpu.make_async_remote_copy(
                src_ref=to_next.at[pl.ds(spot, size)],
                dst_ref=from_prev.at[pl.ds(spot, size)],
                send_sem=next_send.at[turn],
                recv_sem=next_recv.at[turn],
                device_id=(lax.rem(me + 1, n),),
                device_id_type=MESH,
            )
        return pltpu.make_async_remote_copy(
            src_ref=to_prev.at[pl.ds(spot, size)],
            dst_ref=from_next.at[pl.ds(spot, size)],
            send_sem=prev_send.at[turn],
            recv_sem=prev_recv.at[turn],
            device_id=(lax.rem(me + n - 1, n),),
            device_id_type=MESH,
        )

    has_next = me < n - 1
    has_prev = me > 0

    def send(sums, turn):
        spot = FIRST_ROWS[turn]
        for index, member in enumerate(sums):
            to_next[spot + index] = member[:, :LANES]
            to_prev[spot + index] = member[:, LANES:]

        @pl.when(has_next)
        def _():
            neighbour("next", turn, len(sums)).start()

        @pl.when(has_prev)
        def _():
            neighbour("prev", turn, len(sums)).start()

    edge_row = iota((GROUP, LANES), 0) < 2 * edge

    def receive(sums, turn):
        spot = FIRST_ROWS[turn]
        @pl.when(has_next)
        def _():
            copy = neighbour("next", turn, len(sums))
            copy.wait_send()
            neighbour("prev", turn, len(sums)).wait_recv()

        @pl.when(has_prev)
        def _():
            copy = neighbour("prev", turn, len(sums))
            copy.wait_send()
            neighbour("next", turn, len(sums)).wait_recv()

        return [
            jnp.concatenate(
                [
                    member[:, :LANES] + jnp.where(edge_row, from_next[spot + index], 0.0),
                    member[:, LANES:] + jnp.where(edge_row, from_prev[spot + index], 0.0),
                ],
                axis=1,
            )
            for index, member in enumerate(sums)
        ]

    def jac(index):
        return cam_jac[index].astype(F32)

    def pjac(index):
        return point_jac[index].astype(F32)

    def errors_of(vector):
        rows = []
        for side in range(2):
            running = jac(9 * side) * vector[0]
            for entry in range(1, 9):
                running = running + jac(9 * side + entry) * vector[entry]
            rows.append(jnp.where(used, running, 0.0))
        return rows

    def products(errors):
        return [errors[0] * pjac(entry) + errors[1] * pjac(3 + entry) for entry in range(3)]

    def finish(vector, errors, sums):
        values = apply_inverse(inverse, sums)
        terms = [splits_of(value) for value in values]
        stacked = jnp.concatenate(
            [terms[index][step] for step in range(SPLITS) for index in range(3)], axis=0
        ).astype(BF16)
        rows = 3 * GROUP
        for cam in range(cams):
            found = jnp.dot(
                stacked,
                lane_hot[:, cam * slots : (cam + 1) * slots],
                preferred_element_type=F32,
            )
            whole = found[(SPLITS - 1) * rows :]
            for step in reversed(range(SPLITS - 1)):
                whole = whole + found[step * rows : (step + 1) * rows]
            mask = group_row == group_of[cam : cam + 1]
            for index in range(3):
                picked[index, cam : cam + 1] = jnp.sum(
                    jnp.where(mask, whole[index * GROUP : (index + 1) * GROUP], 0.0),
                    axis=0,
                    keepdims=True,
                )
        adjusted = []
        for side in range(2):
            back = picked[0] * pjac(3 * side)
            back = back + picked[1] * pjac(3 * side + 1)
            back = back + picked[2] * pjac(3 * side + 2)
            adjusted.append(errors[side] - back)
        return [
            damp * vector[entry]
            + jnp.sum(
                jac(entry) * adjusted[0] + jac(9 + entry) * adjusted[1], axis=1, keepdims=True
            )
            for entry in range(9)
        ]

    def dot_of(left, right):
        running = left[0] * right[0]
        for entry in range(1, 9):
            running = running + left[entry] * right[entry]
        return jnp.sum(running, axis=0, keepdims=True)

    dot_lane = iota((1, LANES), 1)

    def dots_copy(which, offset):
        return pltpu.make_async_remote_copy(
            src_ref=dots_out.at[which],
            dst_ref=dots_in.at[which, offset - 1],
            send_sem=dots_send.at[which],
            recv_sem=dots_recv.at[which],
            device_id=(lax.rem(me + offset, n),),
            device_id_type=MESH,
        )

    def send_dots(which, members):
        packed = jnp.zeros((1, LANES), F32)
        for index, member in enumerate(members):
            packed = jnp.where(dot_lane == index, member, packed)
        dots_out[which] = packed

        def one(offset, carry):
            dots_copy(which, offset).start()
            return carry

        lax.fori_loop(1, n, one, 0)
        return packed

    def receive_dots(which, packed, count):
        pltpu.make_async_copy(dots_in.at[which], dots_in.at[which], dots_recv.at[which]).wait()
        pltpu.make_async_copy(dots_in.at[which], dots_in.at[which], dots_send.at[which]).wait()
        whole = packed + jnp.sum(dots_in[which], axis=0)
        return [
            jnp.sum(jnp.where(dot_lane == index, whole, 0.0), axis=1, keepdims=True)
            for index in range(count)
        ]

    damp = column(cam_damp[...])
    start = [column(start_guess[entry : entry + 1]) for entry in range(9)]
    right = [column(right_side[entry : entry + 1]) for entry in range(9)]

    errors = errors_of(start)
    blocks = [
        pjac(lead) * pjac(tail) + pjac(3 + lead) * pjac(3 + tail) for lead, tail in ENTRY_PAIRS
    ]
    sums = point_sums(blocks + products(errors))

    damping = jnp.zeros((SPLITS * GROUP, WIDE), F32)
    damp_row = iota((GROUP, WIDE), 0)
    square_row = iota((WIDE, WIDE), 0)
    for index in range(own_groups):
        here = point_damp[:, index * WIDE : (index + 1) * WIDE]
        mask = damp_row == table_group[index : index + 1].astype(I32)
        block = jnp.concatenate([jnp.where(mask, term, 0.0) for term in splits_of(here)], axis=0)
        hot = jnp.where(
            square_row == table_lane[index : index + 1].astype(I32), 1.0, 0.0
        ).astype(BF16)
        damping = damping + dot_nt(block.astype(BF16), hot)
    moved = damping[(SPLITS - 1) * GROUP :]
    for step in reversed(range(SPLITS - 1)):
        moved = moved + damping[step * GROUP : (step + 1) * GROUP]
    for index, (lead, tail) in enumerate(ENTRY_PAIRS):
        if lead == tail:
            sums[index] = sums[index] + moved

    pl.semaphore_wait(barrier, n - 1)
    send(sums, 0)

    precond = []
    for entry in range(9):
        squared = jnp.where(used, jac(entry) ** 2 + jac(9 + entry) ** 2, 0.0)
        precond.append(1.0 / (jnp.sum(squared, axis=1, keepdims=True) + damp))

    sums = receive(sums, 0)
    inverse = symmetric_inverse(sums[:6])
    image = finish(start, errors, sums[6:])
    residual = [right[entry] - image[entry] for entry in range(9)]
    direction = [precond[entry] * residual[entry] for entry in range(9)]

    errors = errors_of(direction)
    sums = point_sums(products(errors))
    send(sums, 1)
    sums = receive(sums, 1)
    image = finish(direction, errors, sums)

    first = send_dots(0, [dot_of(residual, direction), dot_of(direction, image)])
    ahead = [precond[entry] * image[entry] for entry in range(9)]
    errors = errors_of(ahead)
    sums = point_sums(products(errors))
    send(sums, 2)
    sums = receive(sums, 2)
    further = finish(ahead, errors, sums)

    inner, curve = receive_dots(0, first, 2)
    step = inner / curve
    solution = [start[entry] + step * direction[entry] for entry in range(9)]
    residual = [residual[entry] - step * image[entry] for entry in range(9)]
    scaled = [precond[entry] * residual[entry] for entry in range(9)]
    applied = [image[entry] - step * further[entry] for entry in range(9)]
    second = send_dots(
        1,
        [
            dot_of(residual, scaled),
            dot_of(scaled, applied),
            dot_of(scaled, image) + dot_of(direction, applied),
        ],
    )
    inner_next, own_curve, cross = receive_dots(1, second, 3)
    ratio = inner_next / inner
    curve = own_curve + ratio * (cross + ratio * curve)
    step = inner_next / curve
    for entry in range(9):
        fresh = scaled[entry] + ratio * direction[entry]
        seen = applied[entry] + ratio * image[entry]
        step_out[entry : entry + 1] = line(solution[entry] + step * fresh)
        residual_out[entry : entry + 1] = line(residual[entry] - step * seen)


def solution(mesh):
    n = mesh.shape["seg"]

    def shards(
        cam_jac,
        point_jac,
        obs_point,
        obs_count,
        back_list,
        front_list,
        point_damp,
        cam_damp,
        right_side,
        start_guess,
    ):
        cams, slots = obs_point.shape
        observations = cams * slots
        vector = jax.ShapeDtypeStruct(right_side.shape, F32)
        return pl.pallas_call(
            functools.partial(kernel, n),
            out_shape=(vector, vector),
            in_specs=[pl.BlockSpec(memory_space=pltpu.VMEM)] * 10,
            out_specs=(pl.BlockSpec(memory_space=pltpu.VMEM),) * 2,
            scratch_shapes=[
                pltpu.VMEM((WIDE, observations), BF16),
                pltpu.VMEM((SPLITS * 9 * GROUP, observations), BF16),
                pltpu.VMEM((cams, slots), I32),
                pltpu.VMEM((3, cams, slots), F32),
                pltpu.VMEM((15, GROUP, LANES), F32),
                pltpu.VMEM((15, GROUP, LANES), F32),
                pltpu.VMEM((15, GROUP, LANES), F32),
                pltpu.VMEM((15, GROUP, LANES), F32),
                pltpu.VMEM((2, 1, LANES), F32),
                pltpu.VMEM((2, n - 1, 1, LANES), F32),
                pltpu.SemaphoreType.DMA((3,)),
                pltpu.SemaphoreType.DMA((3,)),
                pltpu.SemaphoreType.DMA((3,)),
                pltpu.SemaphoreType.DMA((3,)),
                pltpu.SemaphoreType.DMA((2,)),
                pltpu.SemaphoreType.DMA((2,)),
            ],
            compiler_params=pltpu.CompilerParams(
                collective_id=0, has_side_effects=True, vmem_limit_bytes=48 * 1024 * 1024
            ),
            name="schur_cg",
        )(
            cam_jac,
            point_jac,
            obs_point,
            obs_count.reshape(1, -1),
            back_list,
            front_list,
            point_damp.reshape(1, -1),
            cam_damp.reshape(1, -1),
            right_side,
            start_guess,
        )

    return jax.shard_map(
        shards,
        mesh=mesh,
        in_specs=(
            P(None, "seg", None),
            P(None, "seg", None),
            P("seg", None),
            P("seg"),
            P("seg", None),
            P("seg", None),
            P("seg"),
            P("seg"),
            P(None, "seg"),
            P(None, "seg"),
        ),
        out_specs=(P(None, "seg"), P(None, "seg")),
        check_vma=False,
    )
```

time: 1010 us -> 39.4 us (0.04); the launches traced: 998 us -> 39 us
  other arithmetic: 728 us -> 0 us
  local copies, waits for them, and re-layouts: 132 us -> 7.87 us
  blocking collectives: 120 us -> 0 us
  Pallas kernels: 0 us -> 30.5 us
  starting transfers between devices: 12.1 us -> 0 us
    scatter-add x23 -> x0, other arithmetic: 719 us -> none  [the longest x9 417 us: operator(): jax.ops.segment_sum(product.reshape(-1), owners, num_segments=extended)]
    psum x3 -> x0, blocking collectives: 120 us -> none  [the longest x2 81.3 us: squares(): return lax.psum(jnp.sum(residual * scaled), 'seg')]
    gather x19 -> x0, local copies, waits for them, and re-layouts: 92.8 us -> none  [the longest x3 83.1 us: operator(): picked = values[:, owners].reshape(3, cameras, slot_total)]
    slice x17 -> x0, local copies, waits for them, and re-layouts: 31.8 us -> none  [the longest x3 30.5 us: operator(): picked[2] * point_jac[3 * row_index + 2].astype(jnp.float32)]
    pallas_call x0 -> x1, Pallas kernels: none -> 30.5 us  [shards(): pl.pallas_call(functools.partial(kernel, n), out_shape=(vector, vector),...]
    ppermute x8 -> x0, starting transfers between devices: 12.1 us -> none  [the longest x4 6.95 us: padded(): lax.ppermute(lax.slice_in_dim(block, block.shape[dim] - width, None, axis...]
  transfers between devices with their start and end apart: 8 -> 0, of which waited for: 0 -> 0; matrix products, arithmetic and copies ran while one was open for 16% -> 0% of each run, Pallas kernels for 0% -> 0%
where the time goes in v1:
time: 39.4 us; the launch traced here: 39 us
  Pallas kernels  30.5 us (77%)
  local copies, waits for them, and re-layouts  7.87 us (20%)
  between operations  0.67 us (2%)
    pallas_call x1, Pallas kernels, shards(): pl.pallas_call(functools.partial(kernel, n), out_shape=(vector, vector),...  30.5 us
    unnamed x22, local copies, waits for them, and re-layouts  7.87 us

profile of v1, /device:TPU:0, one launch (start us, length us, event | category | flops | bytes accessed | tf_op | source)
XLA Modules:
  0.0 39.0 jit_solution(10064427629986483558)
XLA Ops:
  0.6 0.0 copy-start.5
  0.6 0.0 copy-start.6
  0.7 0.7 %copy-done.5 = f32[1024]{0:T(1024)S(1)} copy-done((f32[1024]{0:T(1024)S(1)}, f32[1024]{0:T(1024)}, u32[]{:S(2)}) %copy-start.5) | copy-done | bytes 4120
  1.3 0.0 copy-done.6
  1.3 0.0 copy-start
  1.3 1.0 %copy-done = bf16[18,16,512]{2,1,0:T(8,128)(2,1)S(1)} copy-done((bf16[18,16,512]{2,1,0:T(8,128)(2,1)S(1)}, bf16[18,16,512]{2,1,0:T(8,128)(2,1)}, u32[]{:S(2)}) %copy-start) | copy-done | bytes 294936
  2.3 0.0 copy-start.1
  2.3 0.9 %copy-done.1 = bf16[6,16,512]{2,1,0:T(8,128)(2,1)S(1)} copy-done((bf16[6,16,512]{2,1,0:T(8,128)(2,1)S(1)}, bf16[6,16,512]{2,1,0:T(8,128)(2,1)}, u32[]{:S(2)}) %copy-start.1) | copy-done | bytes 98328
  3.2 0.0 copy-start.2
  3.2 0.8 %copy-done.2 = s32[16,512]{1,0:T(8,128)S(1)} copy-done((s32[16,512]{1,0:T(8,128)S(1)}, s32[16,512]{1,0:T(8,128)}, u32[]{:S(2)}) %copy-start.2) | copy-done | bytes 32792
  3.9 0.0 copy-start.3
  3.9 0.7 %copy-done.3 = f32[9,16]{1,0:T(8,128)S(1)} copy-done((f32[9,16]{1,0:T(8,128)S(1)}, f32[9,16]{1,0:T(8,128)}, u32[]{:S(2)}) %copy-start.3) | copy-done | bytes 600
  4.6 0.0 copy-start.4
  4.6 0.7 %copy-done.4 = f32[9,16]{1,0:T(8,128)S(1)} copy-done((f32[9,16]{1,0:T(8,128)S(1)}, f32[9,16]{1,0:T(8,128)}, u32[]{:S(2)}) %copy-start.4) | copy-done | bytes 600
  5.3 0.0 copy-start.7
  5.3 0.7 %copy-done.7 = s32[1,384]{1,0:T(1,128)S(1)} copy-done((s32[1,384]{1,0:T(1,128)S(1)}, s32[1,384]{1,0:T(1,128)}, u32[]{:S(2)}) %copy-start.7) | copy-done | bytes 1560
  6.0 0.0 copy-start.8
  6.0 0.7 %copy-done.8 = s32[16]{0:T(128)S(1)} copy-done((s32[16]{0:T(128)S(1)}, s32[16]{0:T(128)}, u32[]{:S(2)}) %copy-start.8) | copy-done | bytes 88
  6.7 0.0 copy-start.9
  6.7 0.7 %copy-done.9 = f32[16]{0:T(128)S(1)} copy-done((f32[16]{0:T(128)S(1)}, f32[16]{0:T(128)}, u32[]{:S(2)}) %copy-start.9) | copy-done | bytes 88
  7.3 30.5 %schur_cg.1 = (f32[9,16]{1,0:T(8,128)S(1)}, f32[9,16]{1,0:T(8,128)S(1)}) custom-call(bf16[18,16,512]{2,1,0:T(8,128)(2,1)S(1)} %copy-done, bf16[6,16,512]{2,1,0:T(8,128)(2,1)S(1)} %copy-done.1, s32[16,512]{1,0:T(8,128)S(1)} %copy-done.2, s32[1,16]{1,0:T(1,128)S(1)} %bitcast.4, s32[1,384]{1,0:T(1,128)S(1)} %copy-done.6, s32[1,384]{1,0:T(1,128)S(1)} %copy-done.7, ...), custom_call_target="tpu_custom_call" | custom-call | tf_op jit(solution)/shard_map/schur_cg/pallas_call | solution.py:461
  37.8 0.6 %copy.14 = f32[9,16]{1,0:T(8,128)} copy(f32[9,16]{1,0:T(8,128)S(1)} %get-tuple-element.4) | data formatting | bytes 1152
  38.4 0.6 %copy.15 = f32[9,16]{1,0:T(8,128)} copy(f32[9,16]{1,0:T(8,128)S(1)} %get-tuple-element.5) | data formatting | bytes 1152
Async XLA Ops:
  0.6 0.7 %copy-start.5 = (f32[1024]{0:T(1024)S(1)}, f32[1024]{0:T(1024)}, u32[]{:S(2)}) copy-start(f32[1024]{0:T(1024)} %param.16) | copy-start | bytes 12292
  0.6 0.7 %copy-start.6 = (s32[1,384]{1,0:T(1,128)S(1)}, s32[1,384]{1,0:T(1,128)}, u32[]{:S(2)}) copy-start(s32[1,384]{1,0:T(1,128)} %back_list.1) | copy-start | bytes 4612
  1.3 1.0 %copy-start = (bf16[18,16,512]{2,1,0:T(8,128)(2,1)S(1)}, bf16[18,16,512]{2,1,0:T(8,128)(2,1)}, u32[]{:S(2)}) copy-start(bf16[18,16,512]{2,1,0:T(8,128)(2,1)} %cam_jac.1) | copy-start | bytes 884740
  2.3 0.9 %copy-start.1 = (bf16[6,16,512]{2,1,0:T(8,128)(2,1)S(1)}, bf16[6,16,512]{2,1,0:T(8,128)(2,1)}, u32[]{:S(2)}) copy-start(bf16[6,16,512]{2,1,0:T(8,128)(2,1)} %point_jac.1) | copy-start | bytes 294916
  3.2 0.8 %copy-start.2 = (s32[16,512]{1,0:T(8,128)S(1)}, s32[16,512]{1,0:T(8,128)}, u32[]{:S(2)}) copy-start(s32[16,512]{1,0:T(8,128)} %obs_point.1) | copy-start | bytes 98308
  3.9 0.7 %copy-start.3 = (f32[9,16]{1,0:T(8,128)S(1)}, f32[9,16]{1,0:T(8,128)}, u32[]{:S(2)}) copy-start(f32[9,16]{1,0:T(8,128)} %right_side.1) | copy-start | bytes 1732
  4.6 0.7 %copy-start.4 = (f32[9,16]{1,0:T(8,128)S(1)}, f32[9,16]{1,0:T(8,128)}, u32[]{:S(2)}) copy-start(f32[9,16]{1,0:T(8,128)} %start_guess.1) | copy-start | bytes 1732
  5.3 0.7 %copy-start.7 = (s32[1,384]{1,0:T(1,128)S(1)}, s32[1,384]{1,0:T(1,128)}, u32[]{:S(2)}) copy-start(s32[1,384]{1,0:T(1,128)} %front_list.1) | copy-start | bytes 4612
  6.0 0.7 %copy-start.8 = (s32[16]{0:T(128)S(1)}, s32[16]{0:T(128)}, u32[]{:S(2)}) copy-start(s32[16]{0:T(128)} %param.13) | copy-start | bytes 196
  6.7 0.7 %copy-start.9 = (f32[16]{0:T(128)S(1)}, f32[16]{0:T(128)}, u32[]{:S(2)}) copy-start(f32[16]{0:T(128)} %param.17) | copy-start | bytes 196

commit v2 on v1

--- a/solution.py
+++ b/solution.py
@@ -13,8 +13,20 @@
 LANES = 128
 WIDE = 256
 GROUP = 8
-SPLITS = 3
+SPLITS = 2
 FIRST_ROWS = (0, 9, 12)
+LOAD_ORDER = (
+    "back_list",
+    "front_list",
+    "obs_count",
+    "obs_point",
+    "cam_damp",
+    "start_guess",
+    "right_side",
+    "point_damp",
+    "point_jac",
+    "cam_jac",
+)
 
 
 def splits_of(value):
@@ -58,16 +70,16 @@
 
 def kernel(
     n,
-    cam_jac,
-    point_jac,
-    obs_point,
-    obs_count,
-    back_list,
-    front_list,
-    point_damp,
-    cam_damp,
-    right_side,
-    start_guess,
+    cam_jac_hbm,
+    point_jac_hbm,
+    obs_point_hbm,
+    obs_count_hbm,
+    back_list_hbm,
+    front_list_hbm,
+    point_damp_hbm,
+    cam_damp_hbm,
+    right_side_hbm,
+    start_guess_hbm,
     step_out,
     residual_out,
     lane_hot,
@@ -86,6 +98,17 @@
     prev_recv,
     dots_send,
     dots_recv,
+    cam_jac,
+    point_jac,
+    obs_point,
+    obs_count,
+    back_list,
+    front_list,
+    point_damp,
+    cam_damp,
+    right_side,
+    start_guess,
+    load_sem,
 ):
     cams, slots = obs_point.shape
     points = point_damp.shape[1]
@@ -94,6 +117,21 @@
     own_groups = points // WIDE
     me = lax.axis_index("seg")
 
+    loads = {
+        "cam_jac": pltpu.make_async_copy(cam_jac_hbm, cam_jac, load_sem.at[0]),
+        "point_jac": pltpu.make_async_copy(point_jac_hbm, point_jac, load_sem.at[1]),
+        "obs_point": pltpu.make_async_copy(obs_point_hbm, obs_point, load_sem.at[2]),
+        "obs_count": pltpu.make_async_copy(obs_count_hbm, obs_count, load_sem.at[3]),
+        "back_list": pltpu.make_async_copy(back_list_hbm, back_list, load_sem.at[4]),
+        "front_list": pltpu.make_async_copy(front_list_hbm, front_list, load_sem.at[5]),
+        "point_damp": pltpu.make_async_copy(point_damp_hbm, point_damp, load_sem.at[6]),
+        "cam_damp": pltpu.make_async_copy(cam_damp_hbm, cam_damp, load_sem.at[7]),
+        "right_side": pltpu.make_async_copy(right_side_hbm, right_side, load_sem.at[8]),
+        "start_guess": pltpu.make_async_copy(start_guess_hbm, start_guess, load_sem.at[9]),
+    }
+    for name in LOAD_ORDER:
+        loads[name].start()
+
     barrier = pltpu.get_barrier_semaphore()
 
     def greet(offset, carry):
@@ -106,6 +144,8 @@
     from_next[...] = jnp.zeros_like(from_next)
     lax.fori_loop(1, n, greet, 0)
 
+    loads["back_list"].wait()
+    loads["front_list"].wait()
     listed = jnp.concatenate([back_list[...], front_list[...]], axis=1)
     total = 2 * border
     place = iota((1, total), 1)
@@ -146,6 +186,8 @@
         wide = jnp.broadcast_to(col, (cams, cams))
         return jnp.sum(jnp.where(eye, wide, 0.0), axis=0, keepdims=True)
 
+    loads["obs_count"].wait()
+    loads["obs_point"].wait()
     used_count = column(obs_count[...].astype(F32)).astype(I32)
     used = iota((cams, slots), 1) < used_count
 
@@ -282,8 +324,7 @@
     def products(errors):
         return [errors[0] * pjac(entry) + errors[1] * pjac(3 + entry) for entry in range(3)]
 
-    def finish(vector, errors, sums):
-        values = apply_inverse(inverse, sums)
+    def finish(vector, errors, values):
         terms = [splits_of(value) for value in values]
         stacked = jnp.concatenate(
             [terms[index][step] for step in range(SPLITS) for index in range(3)], axis=0
@@ -359,6 +400,8 @@
             for index in range(count)
         ]
 
+    for name in LOAD_ORDER[4:]:
+        loads[name].wait()
     damp = column(cam_damp[...])
     start = [column(start_guess[entry : entry + 1]) for entry in range(9)]
     right = [column(right_side[entry : entry + 1]) for entry in range(9)]
@@ -397,7 +440,7 @@
 
     sums = receive(sums, 0)
     inverse = symmetric_inverse(sums[:6])
-    image = finish(start, errors, sums[6:])
+    image = finish(start, errors, apply_inverse(inverse, sums[6:]))
     residual = [right[entry] - image[entry] for entry in range(9)]
     direction = [precond[entry] * residual[entry] for entry in range(9)]
 
@@ -405,33 +448,48 @@
     sums = point_sums(products(errors))
     send(sums, 1)
     sums = receive(sums, 1)
-    image = finish(direction, errors, sums)
+    values = apply_inverse(inverse, sums)
+    image = finish(direction, errors, values)
 
     first = send_dots(0, [dot_of(residual, direction), dot_of(direction, image)])
     ahead = [precond[entry] * image[entry] for entry in range(9)]
-    errors = errors_of(ahead)
-    sums = point_sums(products(errors))
-    send(sums, 2)
-    sums = receive(sums, 2)
-    further = finish(ahead, errors, sums)
+    errors_ahead = errors_of(ahead)
+    sums_ahead = point_sums(products(errors_ahead))
+    send(sums_ahead, 2)
+    sums_ahead = receive(sums_ahead, 2)
+    values_ahead = apply_inverse(inverse, sums_ahead)
 
     inner, curve = receive_dots(0, first, 2)
     step = inner / curve
     solution = [start[entry] + step * direction[entry] for entry in range(9)]
     residual = [residual[entry] - step * image[entry] for entry in range(9)]
     scaled = [precond[entry] * residual[entry] for entry in range(9)]
+
+    quadratic = jnp.zeros((cams, 1), F32)
+    for entry in range(9):
+        quadratic = quadratic + damp * scaled[entry] * scaled[entry]
+    squares = (errors[0] - step * errors_ahead[0]) ** 2 + (errors[1] - step * errors_ahead[1]) ** 2
+    quadratic = quadratic + jnp.sum(squares, axis=1, keepdims=True)
+    quadratic = jnp.sum(quadratic, axis=0, keepdims=True)
+    point_part = jnp.zeros((GROUP, WIDE), F32)
+    for index in range(3):
+        point_part = point_part + (sums[index] - step * sums_ahead[index]) * (
+            values[index] - step * values_ahead[index]
+        )
+    part_row = iota((GROUP, WIDE), 0)
+    part_left = iota((GROUP, WIDE), 1) < LANES
+    own_row = jnp.where(part_left, part_row, part_row - edge)
+    is_own = jnp.where(part_left, edge - 1 - own_row, own_row) >= 0
+    is_own = is_own | (part_row >= 2 * edge)
+    point_part = jnp.sum(jnp.where(is_own, point_part, 0.0), axis=1, keepdims=True)
+    quadratic = quadratic - jnp.sum(point_part, axis=0, keepdims=True)
+    second = send_dots(1, [dot_of(residual, scaled), quadratic, dot_of(scaled, image)])
+
+    further = finish(ahead, errors_ahead, values_ahead)
     applied = [image[entry] - step * further[entry] for entry in range(9)]
-    second = send_dots(
-        1,
-        [
-            dot_of(residual, scaled),
-            dot_of(scaled, applied),
-            dot_of(scaled, image) + dot_of(direction, applied),
-        ],
-    )
     inner_next, own_curve, cross = receive_dots(1, second, 3)
     ratio = inner_next / inner
-    curve = own_curve + ratio * (cross + ratio * curve)
+    curve = own_curve + ratio * (2.0 * cross + ratio * curve)
     step = inner_next / curve
     for entry in range(9):
         fresh = scaled[entry] + ratio * direction[entry]
@@ -457,11 +515,23 @@
     ):
         cams, slots = obs_point.shape
         observations = cams * slots
+        operands = (
+            cam_jac,
+            point_jac,
+            obs_point,
+            obs_count.reshape(1, -1),
+            back_list,
+            front_list,
+            point_damp.reshape(1, -1),
+            cam_damp.reshape(1, -1),
+            right_side,
+            start_guess,
+        )
         vector = jax.ShapeDtypeStruct(right_side.shape, F32)
         return pl.pallas_call(
             functools.partial(kernel, n),
             out_shape=(vector, vector),
-            in_specs=[pl.BlockSpec(memory_space=pltpu.VMEM)] * 10,
+            in_specs=[pl.BlockSpec(memory_space=pltpu.HBM)] * 10,
             out_specs=(pl.BlockSpec(memory_space=pltpu.VMEM),) * 2,
             scratch_shapes=[
                 pltpu.VMEM((WIDE, observations), BF16),
@@ -480,23 +550,14 @@
                 pltpu.SemaphoreType.DMA((3,)),
                 pltpu.SemaphoreType.DMA((2,)),
                 pltpu.SemaphoreType.DMA((2,)),
+                *[pltpu.VMEM(member.shape, member.dtype) for member in operands],
+                pltpu.SemaphoreType.DMA((len(operands),)),
             ],
             compiler_params=pltpu.CompilerParams(
-                collective_id=0, has_side_effects=True, vmem_limit_bytes=48 * 1024 * 1024
+                collective_id=0, has_side_effects=True, vmem_limit_bytes=56 * 1024 * 1024
             ),
             name="schur_cg",
-        )(
-            cam_jac,
-            point_jac,
-            obs_point,
-            obs_count.reshape(1, -1),
-            back_list,
-            front_list,
-            point_damp.reshape(1, -1),
-            cam_damp.reshape(1, -1),
-            right_side,
-            start_guess,
-        )
+        )(*operands)
 
     return jax.shard_map(
         shards,

time: 39.4 us -> 33.9 us (0.86)
  local copies, waits for them, and re-layouts: 7.87 us -> 1.9 us
  Pallas kernels: 30.5 us -> 31.2 us
    unnamed x22 -> x4, local copies, waits for them, and re-layouts: 7.87 us -> 1.9 us
    pallas_call x1, Pallas kernels: 30.5 us -> 31.2 us  [shards(): pl.pallas_call(functools.partial(kernel, n), out_shape=(vector, vector),...]
where the time goes in v2:
time: 33.9 us; the launch traced here: 33.8 us
  Pallas kernels  31.2 us (92%)
  local copies, waits for them, and re-layouts  1.9 us (6%)
  between operations  0.65 us (2%)
    pallas_call x1, Pallas kernels, shards(): pl.pallas_call(functools.partial(kernel, n), out_shape=(vector, vector),...  31.2 us
    unnamed x4, local copies, waits for them, and re-layouts  1.9 us

profile of v2, /device:TPU:0, one launch (start us, length us, event | category | flops | bytes accessed | tf_op | source)
XLA Modules:
  0.0 33.8 jit_solution(13172873067423832041)
XLA Ops:
  0.6 31.2 %schur_cg.1 = (f32[9,16]{1,0:T(8,128)}, f32[9,16]{1,0:T(8,128)}) custom-call(bf16[18,16,512]{2,1,0:T(8,128)(2,1)} %cam_jac_hbm.1, bf16[6,16,512]{2,1,0:T(8,128)(2,1)} %point_jac_hbm.1, s32[16,512]{1,0:T(8,128)} %obs_point_hbm.1, s32[1,16]{1,0:T(1,128)} %bitcast.4, s32[1,384]{1,0:T(1,128)} %back_list_hbm.1, s32[1,384]{1,0:T(1,128)} %front_list_hbm.1, ...), custom_call_target="tpu_custom_call" | custom-call | tf_op jit(solution)/shard_map/schur_cg/pallas_call | solution.py:531
  31.9 0.0 copy-start
  31.9 1.3 %copy.14 = f32[9,16]{1,0:T(8,128)} copy(f32[9,16]{1,0:T(8,128)} %get-tuple-element.4) | data formatting | bytes 1152
  33.2 0.0 copy-done
  33.2 0.6 %copy.15 = f32[9,16]{1,0:T(8,128)} copy(f32[9,16]{1,0:T(8,128)S(1)} %copy-done) | data formatting | bytes 1152
Async XLA Ops:
  31.9 1.3 %copy-start = (f32[9,16]{1,0:T(8,128)S(1)}, f32[9,16]{1,0:T(8,128)}, u32[]{:S(2)}) copy-start(f32[9,16]{1,0:T(8,128)} %get-tuple-element.5) | copy-start | bytes 1732
